TPU v7x, 32 devices: a whole 2x2x4 slice. The times are simulated.
32 devices in a mesh: wide: 8 (over y, x, core), narrow: 4 (over z).
Axes of the slice: x: 2, y: 2, z: 4, core: 2. Of those that a mesh axis runs over, the one named last changes fastest.
Arguments:
- left: bfloat16 [32, 32, 256], P('narrow', None, 'wide'), may hold values from -6 to 6
- right: bfloat16 [32, 32, 256], P('wide', None, 'narrow'), may hold values from -6 to 6
- out_weight: bfloat16 [1024, 128], replicated, may hold values from -1 to 1
- out_bias: float32 [128], replicated, may hold values from -3 to 3
- cotangent: bfloat16 [256, 256, 128], P('wide', 'narrow'), may hold values from -0.5 to 0.5
Outputs:
- pair_update: bfloat16 [256, 256, 128], P('wide', 'narrow')
- grad_left: float32 [32, 32, 256], P('narrow', None, 'wide')
- grad_right: float32 [32, 32, 256], P('wide', None, 'narrow')
All inputs are finite; a program needn't handle non-finite values.
Results may differ from a plain program's by a relative error of at most 0.0045.
Values may be sent and summed in bfloat16 or wider, within the bound.
No kernel may reach another device: no remote copies, remote signals or barrier semaphores. Data moves between devices by JAX's collectives and lax.ppermute only.
A program may use at most 64 MiB of HBM per device.

v0:
```python
import math
import jax
import jax.numpy as jnp
from jax import lax
from jax.sharding import PartitionSpec as P


def local(left, right, out_weight, out_bias, cotangent):
    left_complete = lax.all_gather(left, "narrow", axis=0, tiled=True)
    right_full = lax.all_gather(right, "wide", axis=0, tiled=True)
    alignment_rows = left_complete.shape[0]
    channel_count = left_complete.shape[1]
    tile_rows = left_complete.shape[2]
    tile_columns = right_full.shape[2]
    pair_width = cotangent.shape[2]
    rows_per_block = math.gcd(16, tile_rows)
    total_block_count = tile_rows // rows_per_block
    kept_rows = alignment_rows // lax.axis_size("narrow")

    def block_step(block_index, carry):
        running, pairs, grads = carry
        start = (block_index * rows_per_block).astype(jnp.int32)
        left_block = lax.dynamic_slice_in_dim(left_complete, start, rows_per_block, 2)
        cot_block = lax.dynamic_slice_in_dim(cotangent, start, rows_per_block, 0)
        outer_sum = (
            jnp.einsum("sci,sej->ijce", left_block, right_full, preferred_element_type=jnp.float32)
            / alignment_rows
        )
        outer_flat = outer_sum.astype(jnp.bfloat16).reshape(
            rows_per_block * tile_columns, channel_count * channel_count
        )
        pair_out = jnp.dot(outer_flat, out_weight, preferred_element_type=jnp.float32) + out_bias
        pair_out = pair_out.astype(jnp.bfloat16).reshape(rows_per_block, tile_columns, pair_width)
        cot_flat = cot_block.reshape(rows_per_block * tile_columns, pair_width)
        d_outer = lax.dot_general(
            cot_flat, out_weight, (((1,), (1,)), ((), ())), preferred_element_type=jnp.float32
        )
        d_outer = d_outer.astype(jnp.bfloat16).reshape(
            rows_per_block, tile_columns, channel_count, channel_count
        )
        grad_block = (
            jnp.einsum("ijce,sej->sci", d_outer, right_full, preferred_element_type=jnp.float32)
            / alignment_rows
        )
        running = (
            running
            + jnp.einsum("ijce,sci->sej", d_outer, left_block, preferred_element_type=jnp.float32)
            / alignment_rows
        )
        grad_block = lax.psum_scatter(grad_block, "narrow", scatter_dimension=0, tiled=True)
        pairs = lax.dynamic_update_slice_in_dim(pairs, pair_out, start, 0)
        grads = lax.dynamic_update_slice_in_dim(grads, grad_block, start, 2)
        return (running, pairs, grads)

    starting_value = (
        jnp.zeros((alignment_rows, channel_count, tile_columns), jnp.float32),
        jnp.zeros((tile_rows, tile_columns, pair_width), jnp.bfloat16),
        jnp.zeros((kept_rows, channel_count, tile_rows), jnp.float32),
    )
    right_terms, pair_update, grad_terms = lax.fori_loop(
        0, total_block_count, block_step, starting_value
    )
    grad_right = lax.psum_scatter(right_terms, "wide", scatter_dimension=0, tiled=True)
    return (pair_update, grad_terms, grad_right)


def solution(mesh):
    return jax.shard_map(
        local,
        mesh=mesh,
        in_specs=(
            P("narrow", None, "wide"),
            P("wide", None, "narrow"),
            P(),
            P(),
            P("wide", "narrow", None),
        ),
        out_specs=(P("wide", "narrow", None), P("narrow", None, "wide"), P("wide", None, "narrow")),
        check_vma=False,
    )
```

profile of v0, /device:TPU:0, one launch (start us, length us, event | category | flops | bytes accessed | tf_op | source)
XLA Modules:
  0.0 147.1 jit_solution(11280594527067747907)
XLA Ops:
  8.0 0.9 copy.29
  9.0 14.5 %all_gather.6 = bf16[32,32,32]{1,0,2:T(8,128)(2,1)S(1)} all-gather(bf16[8,32,32]{1,0,2:T(8,128)(2,1)S(1)} %copy.29), channel_id=1, replica_groups=mesh['wide'=8,'narrow'=4] {'narrow'}, dimensions={0}, use_global_device_ids=true | all-gather | bytes 81920 | tf_op jit(solution)/shard_map/all_gather | solution.py:9
  23.4 9.5 %all_gather.7 = bf16[32,32,64]{2,1,0:T(8,128)(2,1)S(1)} all-gather(bf16[4,32,64]{2,1,0:T(8,128)(2,1)} %param.8), channel_id=1, replica_groups=mesh['wide'=8,'narrow'=4] {'wide'}, dimensions={0}, use_global_device_ids=true | all-gather | bytes 147456 | tf_op jit(solution)/shard_map/all_gather | solution.py:10
  33.0 0.1 copy.30
  33.1 0.1 broadcast_in_dim.13
  33.2 70.0 %while.18 = (s32[]{:T(128)}, f32[32,32,64]{2,0,1:T(8,128)}, bf16[32,64,128]{2,1,0:T(8,128)(2,1)S(1)}, f32[8,32,32]{1,2,0:T(8,128)S(1)}, bf16[32,32,32]{1,0,2:T(8...) while((s32[]{:T(128)}, f32[32,32,64]{2,0,1:T(8,128)}, ...), condition=%wide.region_2.0_spmd.clone, body=%wide.region_0.0_spmd.clone.sunk | while | flops 741818368 | bytes 32361256 | solution.py:60
  33.2 0.0 reduce-scatter.5.cloned.1.call-start
  33.3 1.0 constant_dynamic-slice_fusion.2
  34.2 3.0 %convolution_convert_fusion.2 = bf16[1024,1024]{1,0:T(8,128)(2,1)} fusion(bf16[1024,128]{1,0:T(8,128)(2,1)S(1)} %bitcast.82, bf16[1024,128]{1,0:T(8,128)(2,1)} %get-tuple-element.315), kind=kOutput, calls=%fused_computation.4.clone.1 | convolution fusion | flops 269484032 | bytes 2621440 | tf_op jit(solution)/shard_map/while/body/eval_jaxpr/dot_general | solution.py:35
  37.2 2.9 %copy.53 = bf16[1024,1024]{0,1:T(8,128)(2,1)S(1)} copy(bf16[1024,1024]{1,0:T(8,128)(2,1)} %convolution_convert_fusion.2) | data formatting | bytes 4194304 | tf_op jit(solution)/shard_map/while/body/eval_jaxpr/convert_element_type | solution.py:38
  40.1 4.0 %reshape.46 = bf16[16,64,32,32]{1,0,3,2:T(8,128)(2,1)} reshape(bf16[1024,1024]{0,1:T(8,128)(2,1)S(1)} %copy.53) | data formatting | bytes 4194304 | tf_op jit(solution)/shard_map/while/body/eval_jaxpr/reshape | solution.py:38
  44.1 3.4 %fusion.58 = f32[32,32,16]{0,2,1:T(8,128)S(1)} fusion(bf16[16,64,32,32]{1,0,3,2:T(8,128)(2,1)} %reshape.46, bf16[32,32,64]{2,0,1:T(8,128)(2,1)S(1)} %get-tuple-element.316), kind=kOutput, calls=%fused_computation.13.clone.1 | convolution fusion | flops 67125248 | bytes 2293760 | tf_op jit(solution)/shard_map/while/body/eval_jaxpr/ijce,sej->sci/dot_general | solution.py:42
  47.5 0.9 copy.55
  48.4 0.0 reduce-scatter.5.cloned.1.call-update
  48.4 1.3 fusion.56
  49.7 4.7 %copy.54 = bf16[16,64,32,32]{1,0,3,2:T(8,128)(2,1)} copy(bf16[16,64,32,32]{1,2,3,0:T(8,128)(2,1)S(1)} %fusion.56) | data formatting | bytes 4194304 | tf_op jit(solution)/shard_map/while/body/eval_jaxpr/convert_element_type | solution.py:29
  54.4 5.5 %reshape.47 = bf16[1024,1024]{0,1:T(8,128)(2,1)S(1)} reshape(bf16[16,64,32,32]{1,0,3,2:T(8,128)(2,1)} %copy.54) | data formatting | bytes 4194304 | tf_op jit(solution)/shard_map/while/body/eval_jaxpr/reshape | solution.py:29
  59.8 0.0 copy-start
  59.8 0.0 copy-start.2
  59.9 5.7 %fusion.55 = f32[32,32,64]{2,0,1:T(8,128)} fusion(bf16[16,64,32,32]{1,0,3,2:T(8,128)(2,1)} %reshape.46, f32[32,32,64]{2,0,1:T(8,128)} %get-tuple-element.297, pred[]{:T(512)S(6)} %compare.3, bf16[32,32,32]{1,0,2:T(8,128)(2,1)S(1)} %get-tuple-element.313, s32[]{:T(128)S(6)} %select_n.12), kind=kOutput, calls=%fused_computation.9.clone.1 | convolution fusion | flops 67305472 | bytes 2752517 | tf_op jit(solution)/shard_map/while/body/eval_jaxpr/ijce,sci->sej/dot_general | solution.py:47
  65.5 0.0 copy-done
  65.5 0.0 copy-done.2
  65.5 0.7 fusion.57
  66.3 1.6 %reduce-scatter.5.cloned.1.call-done = f32[8,32,16]{1,2,0:T(8,128)} async-done(((f32[32,32,16]{1,2,0:T(8,128)}), f32[8,32,16]{1,2,0:T(8,128)}) %reduce-scatter.5.cloned.1.call-update) | async-done | bytes 16400 | tf_op jit(solution)/shard_map/while/body/eval_jaxpr/reduce_scatter | solution.py:50
  67.9 0.8 constant_dynamic-update-slice_fusion.5
  68.8 0.0 reduce-scatter.5.cloned.1.call-start
  68.8 1.0 constant_dynamic-slice_fusion.2
  69.8 3.0 %convolution_convert_fusion.2 = bf16[1024,1024]{1,0:T(8,128)(2,1)} fusion(bf16[1024,128]{1,0:T(8,128)(2,1)S(1)} %bitcast.82, bf16[1024,128]{1,0:T(8,128)(2,1)} %get-tuple-element.315), kind=kOutput, calls=%fused_computation.4.clone.1 | convolution fusion | flops 269484032 | bytes 2621440 | tf_op jit(solution)/shard_map/while/body/eval_jaxpr/dot_general | solution.py:35
  72.8 2.9 %copy.53 = bf16[1024,1024]{0,1:T(8,128)(2,1)S(1)} copy(bf16[1024,1024]{1,0:T(8,128)(2,1)} %convolution_convert_fusion.2) | data formatting | bytes 4194304 | tf_op jit(solution)/shard_map/while/body/eval_jaxpr/convert_element_type | solution.py:38
  75.6 4.0 %reshape.46 = bf16[16,64,32,32]{1,0,3,2:T(8,128)(2,1)} reshape(bf16[1024,1024]{0,1:T(8,128)(2,1)S(1)} %copy.53) | data formatting | bytes 4194304 | tf_op jit(solution)/shard_map/while/body/eval_jaxpr/reshape | solution.py:38
  79.6 3.4 %fusion.58 = f32[32,32,16]{0,2,1:T(8,128)S(1)} fusion(bf16[16,64,32,32]{1,0,3,2:T(8,128)(2,1)} %reshape.46, bf16[32,32,64]{2,0,1:T(8,128)(2,1)S(1)} %get-tuple-element.316), kind=kOutput, calls=%fused_computation.13.clone.1 | convolution fusion | flops 67125248 | bytes 2293760 | tf_op jit(solution)/shard_map/while/body/eval_jaxpr/ijce,sej->sci/dot_general | solution.py:42
  83.0 0.9 copy.55
  83.9 0.0 reduce-scatter.5.cloned.1.call-update
  83.9 1.3 fusion.56
  85.2 4.7 %copy.54 = bf16[16,64,32,32]{1,0,3,2:T(8,128)(2,1)} copy(bf16[16,64,32,32]{1,2,3,0:T(8,128)(2,1)S(1)} %fusion.56) | data formatting | bytes 4194304 | tf_op jit(solution)/shard_map/while/body/eval_jaxpr/convert_element_type | solution.py:29
  89.9 5.5 %reshape.47 = bf16[1024,1024]{0,1:T(8,128)(2,1)S(1)} reshape(bf16[16,64,32,32]{1,0,3,2:T(8,128)(2,1)} %copy.54) | data formatting | bytes 4194304 | tf_op jit(solution)/shard_map/while/body/eval_jaxpr/reshape | solution.py:29
  95.4 0.0 copy-start
  95.4 0.0 copy-start.2
  95.4 5.8 %fusion.55 = f32[32,32,64]{2,0,1:T(8,128)} fusion(bf16[16,64,32,32]{1,0,3,2:T(8,128)(2,1)} %reshape.46, f32[32,32,64]{2,0,1:T(8,128)} %get-tuple-element.297, pred[]{:T(512)S(6)} %compare.3, bf16[32,32,32]{1,0,2:T(8,128)(2,1)S(1)} %get-tuple-element.313, s32[]{:T(128)S(6)} %select_n.12), kind=kOutput, calls=%fused_computation.9.clone.1 | convolution fusion | flops 67305472 | bytes 2752517 | tf_op jit(solution)/shard_map/while/body/eval_jaxpr/ijce,sci->sej/dot_general | solution.py:47
  101.2 0.0 copy-done
  101.2 0.0 copy-done.2
  101.2 0.7 fusion.57
  102.0 0.4 reduce-scatter.5.cloned.1.call-done
  102.4 0.8 constant_dynamic-update-slice_fusion.5
  103.2 0.0 copy-start.1
  103.2 0.0 reduce-scatter.3.cloned.1.call-start
  103.2 2.3 %copy.31 = f32[32,32,64]{2,1,0:T(8,128)} copy(f32[32,32,64]{2,0,1:T(8,128)} %get-tuple-element.161) | data formatting | bytes 524288 | tf_op jit(solution)/shard_map/while | solution.py:60
  105.6 0.0 reduce-scatter.3.cloned.1.call-update
  105.6 0.8 copy.32
  106.3 33.4 %reduce-scatter.3.cloned.1.call-done = f32[4,32,64]{2,1,0:T(8,128)} async-done(((f32[32,32,64]{2,1,0:T(8,128)}), f32[4,32,64]{2,1,0:T(8,128)}) %reduce-scatter.3.cloned.1.call-update) | async-done | bytes 32784 | tf_op jit(solution)/shard_map/reduce_scatter | solution.py:63
  139.7 0.0 copy-done.1
  (4 shorter events, 0.1 us)
Async XLA Ops:
  33.2 34.7 %reduce-scatter.5.cloned.1.call-start = ((), (), s32[]{:S(2)}) async-start(), calls=%async_computation.3 | async-start | bytes 327680 | tf_op jit(solution)/shard_map/while/body/eval_jaxpr/reduce_scatter | solution.py:50
  59.8 5.7 %copy-start = (bf16[1024,128]{1,0:T(8,128)(2,1)S(1)}, bf16[1024,128]{1,0:T(8,128)(2,1)}, u32[]{:S(2)}) copy-start(bf16[1024,128]{1,0:T(8,128)(2,1)} %get-tuple-element.315) | copy-start | bytes 786436 | tf_op jit(solution)/shard_map/while
  59.8 5.7 %copy-start.2 = (f32[128]{0:T(128)S(1)}, f32[128]{0:T(128)}, u32[]{:S(2)}) copy-start(f32[128]{0:T(128)} %get-tuple-element.317) | copy-start | bytes 1540 | tf_op jit(solution)/shard_map/while
  68.8 33.6 %reduce-scatter.5.cloned.1.call-start = ((), (), s32[]{:S(2)}) async-start(), calls=%async_computation.3 | async-start | bytes 327680 | tf_op jit(solution)/shard_map/while/body/eval_jaxpr/reduce_scatter | solution.py:50
  95.4 5.8 %copy-start = (bf16[1024,128]{1,0:T(8,128)(2,1)S(1)}, bf16[1024,128]{1,0:T(8,128)(2,1)}, u32[]{:S(2)}) copy-start(bf16[1024,128]{1,0:T(8,128)(2,1)} %get-tuple-element.315) | copy-start | bytes 786436 | tf_op jit(solution)/shard_map/while
  95.4 5.8 %copy-start.2 = (f32[128]{0:T(128)S(1)}, f32[128]{0:T(128)}, u32[]{:S(2)}) copy-start(f32[128]{0:T(128)} %get-tuple-element.317) | copy-start | bytes 1540 | tf_op jit(solution)/shard_map/while
  103.2 36.5 %copy-start.1 = (bf16[32,64,128]{2,1,0:T(8,128)(2,1)}, bf16[32,64,128]{2,1,0:T(8,128)(2,1)S(1)}, u32[]{:S(2)}) copy-start(bf16[32,64,128]{2,1,0:T(8,128)(2,1)S(1)} %get-tuple-element.207) | copy-start | bytes 1572868
  103.2 36.5 %reduce-scatter.3.cloned.1.call-start = ((), (), s32[]{:S(2)}) async-start(), calls=%async_computation.2 | async-start | bytes 589824 | tf_op jit(solution)/shard_map/reduce_scatter | solution.py:63
Sparse Core Ops, SparseCore 0:
  48.5 19.3 reduce-scatter.4
  84.0 18.2 reduce-scatter.4
Sparse Core Ops, SparseCore 1:
  107.3 32.3 reduce-scatter.2
where the time goes:
time: 148 us; the launch traced here: 147 us
  local copies, waits for them, and re-layouts  43.7 us (30%)
  waiting for transfers between devices  35.4 us (24%)
  matrix products  28.3 us (19%)
  blocking collectives  24 us (16%)
  between operations  15.5 us (10%)
    reduce_scatter x1, waiting for transfers between devices, local(): lax.psum_scatter(right_terms, 'wide', scatter_dimension=0, tiled=True)  33.4 us
    all_gather x1, blocking collectives, local(): left_complete = lax.all_gather(left, 'narrow', axis=0, tiled=True)  14.5 us
    dot_general x2, matrix products, block_step(): jnp.einsum('ijce,sci->sej', d_outer, left_block, preferred_element_type=j...  11.5 us
    reshape x2, local copies, waits for them, and re-layouts, block_step(): outer_sum.astype(jnp.bfloat16)  10.9 us
    all_gather x1, blocking collectives, local(): right_full = lax.all_gather(right, 'wide', axis=0, tiled=True)  9.51 us
    convert_element_type x2, local copies, waits for them, and re-layouts, block_step(): outer_sum.astype(jnp.bfloat16)  9.33 us
    reshape x2, local copies, waits for them, and re-layouts, block_step(): d_outer.astype(jnp.bfloat16)  7.98 us
    dot_general x2, matrix products, block_step(): jnp.einsum('ijce,sej->sci', d_outer, right_full, preferred_element_type=j...  6.81 us
  transfers between devices with their start and end apart: 3, of which 3 were waited for; matrix products, arithmetic and copies ran while one was open for 25% of the time, Pallas kernels for 0%

commit v1 on v0

--- a/solution.py
+++ b/solution.py
@@ -5,8 +5,18 @@
 from jax.sharding import PartitionSpec as P
 
 
+def pass_along(x, name, along):
+    devices = lax.axis_size(name)
+    held, blocks = (x, [x])
+    for _ in range(devices - 1):
+        held = lax.ppermute(held, name, [(i, (i + 1) % devices) for i in range(devices)])
+        blocks.insert(0, held)
+    line = jnp.concatenate(blocks, axis=along)
+    return jnp.roll(line, (lax.axis_index(name) + 1) * x.shape[along], axis=along)
+
+
 def local(left, right, out_weight, out_bias, cotangent):
-    left_complete = lax.all_gather(left, "narrow", axis=0, tiled=True)
+    left_complete = pass_along(left, "narrow", 0)
     right_full = lax.all_gather(right, "wide", axis=0, tiled=True)
     alignment_rows = left_complete.shape[0]
     channel_count = left_complete.shape[1]

time: 148 us -> 149 us (level)
  blocking collectives: 24 us -> 9.73 us
  waiting for transfers between devices: 35.4 us -> 46.8 us
  starting transfers between devices: 0.08 us -> 3.19 us
    all_gather x1 -> x0, blocking collectives: 14.5 us -> none  [local(): left_complete = lax.all_gather(left, 'narrow', axis=0, tiled=True)]
    ppermute x0 -> x3, waiting for transfers between devices: none -> 10.3 us  [pass_along(): lax.ppermute(held, name, [(i, (i + 1) % devices) for i in range(devices)])]
    ppermute x0 -> x3, starting transfers between devices: none -> 3.11 us  [pass_along(): lax.ppermute(held, name, [(i, (i + 1) % devices) for i in range(devices)])]
  transfers between devices with their start and end apart: 3 -> 6, of which waited for: 3 -> 5; matrix products, arithmetic and copies ran while one was open for 25% -> 25% of each run, Pallas kernels for 0% -> 0%
where the time goes in v1:
time: 149 us; the launch traced here: 148 us
  waiting for transfers between devices  46.8 us (31%)
  local copies, waits for them, and re-layouts  44 us (30%)
  matrix products  28.3 us (19%)
  between operations  15.6 us (10%)
  blocking collectives  9.73 us (7%)
  starting transfers between devices  3.19 us (2%)
    reduce_scatter x1, waiting for transfers between devices, local(): lax.psum_scatter(right_terms, 'wide', scatter_dimension=0, tiled=True)  33.4 us
    dot_general x2, matrix products, block_step(): jnp.einsum('ijce,sci->sej', d_outer, left_block, preferred_element_type=j...  11.5 us
    reshape x2, local copies, waits for them, and re-layouts, block_step(): outer_sum.astype(jnp.bfloat16)  11 us
    ppermute x3, waiting for transfers between devices, pass_along(): lax.ppermute(held, name, [(i, (i + 1) % devices) for i in range(devices)])  10.3 us
    all_gather x1, blocking collectives, local(): right_full = lax.all_gather(right, 'wide', axis=0, tiled=True)  9.73 us
    convert_element_type x2, local copies, waits for them, and re-layouts, block_step(): outer_sum.astype(jnp.bfloat16)  9.37 us
    reshape x2, local copies, waits for them, and re-layouts, block_step(): d_outer.astype(jnp.bfloat16)  8.03 us
    dot_general x2, matrix products, block_step(): jnp.einsum('ijce,sej->sci', d_outer, right_full, preferred_element_type=j...  6.81 us
  transfers between devices with their start and end apart: 6, of which 5 were waited for; matrix products, arithmetic and copies ran while one was open for 25% of the time, Pallas kernels for 0%

profile of v1, /device:TPU:0, one launch (start us, length us, event | category | flops | bytes accessed | tf_op | source)
XLA Modules:
  0.0 147.7 jit_solution(10675459022013286093)
XLA Ops:
  8.0 0.9 copy.33
  8.9 3.1 %collective-permute-start = (bf16[8,32,32]{1,0,2:T(8,128)(2,1)S(1)}, bf16[8,32,32]{1,0,2:T(8,128)(2,1)S(1)}, u32[]{:S(2)}, u32[]{:S(2)}) collective-permute-start(bf16[8,32,32]{1,0,2:T(8,128)(2,1)S(1)} %copy.33), channel_id=1, source_target_pairs={{0,1},{1,2},{2,3},{3,0},{4,5},{5,6},{6,7},{7,4},{8,9},{9,10},{10,1... | collective-permute-start | bytes 49160 | tf_op jit(solution)/shard_map/ppermute | solution.py:12
  12.0 4.3 %collective-permute-done = bf16[8,32,32]{1,0,2:T(8,128)(2,1)S(1)} collective-permute-done((bf16[8,32,32]{1,0,2:T(8,128)(2,1)S(1)}, bf16[8,32,32]{1,0,2:T(8,128)(2,1)S(1)}, u32[]{:S(2)}, u32[]{:S(2)}) %collective-permute-start) | collective-permute-done | bytes 16416 | tf_op jit(solution)/shard_map/ppermute | solution.py:12
  16.3 0.0 collective-permute-start.1
  16.3 6.1 %collective-permute-done.1 = bf16[8,32,32]{1,0,2:T(8,128)(2,1)S(1)} collective-permute-done((bf16[8,32,32]{1,0,2:T(8,128)(2,1)S(1)}, bf16[8,32,32]{1,0,2:T(8,128)(2,1)S(1)}, u32[]{:S(2)}, u32[]{:S(2)}) %collective-permute-start.1) | collective-permute-done | bytes 16416 | tf_op jit(solution)/shard_map/ppermute | solution.py:12
  22.4 0.0 collective-permute-start.2
  22.4 9.7 %all_gather.3 = bf16[32,32,64]{2,1,0:T(8,128)(2,1)S(1)} all-gather(bf16[4,32,64]{2,1,0:T(8,128)(2,1)} %param.8), channel_id=1, replica_groups=mesh['wide'=8,'narrow'=4] {'wide'}, dimensions={0}, use_global_device_ids=true | all-gather | bytes 147456 | tf_op jit(solution)/shard_map/all_gather | solution.py:20
  32.1 0.1 copy.36
  32.2 0.0 collective-permute-done.2
  32.5 0.1 broadcast_in_dim.13
  32.6 71.2 %while.18 = (s32[]{:T(128)}, f32[32,32,64]{2,0,1:T(8,128)}, bf16[32,64,128]{2,1,0:T(8,128)(2,1)S(1)}, f32[8,32,32]{1,2,0:T(8,128)S(1)}, bf16[32,32,32]{1,0,2:T(8...) while((s32[]{:T(128)}, f32[32,32,64]{2,0,1:T(8,128)}, ...), condition=%wide.region_2.3_spmd.clone, body=%wide.region_0.2_spmd.clone.sunk | while | flops 741818368 | bytes 32361256 | solution.py:70
  32.6 0.0 reduce-scatter.5.cloned.1.call-start
  32.7 1.0 constant_dynamic-slice_fusion.3
  33.7 3.0 %convolution_convert_fusion.2 = bf16[1024,1024]{1,0:T(8,128)(2,1)} fusion(bf16[1024,128]{1,0:T(8,128)(2,1)S(1)} %bitcast.82, bf16[1024,128]{1,0:T(8,128)(2,1)} %get-tuple-element.315), kind=kOutput, calls=%fused_computation.4.clone.1 | convolution fusion | flops 269484032 | bytes 2621440 | tf_op jit(solution)/shard_map/while/body/eval_jaxpr/dot_general | solution.py:45
  36.7 2.9 %copy.59 = bf16[1024,1024]{0,1:T(8,128)(2,1)S(1)} copy(bf16[1024,1024]{1,0:T(8,128)(2,1)} %convolution_convert_fusion.2) | data formatting | bytes 4194304 | tf_op jit(solution)/shard_map/while/body/eval_jaxpr/convert_element_type | solution.py:48
  39.5 4.0 %reshape.46 = bf16[16,64,32,32]{1,0,3,2:T(8,128)(2,1)} reshape(bf16[1024,1024]{0,1:T(8,128)(2,1)S(1)} %copy.59) | data formatting | bytes 4194304 | tf_op jit(solution)/shard_map/while/body/eval_jaxpr/reshape | solution.py:48
  43.5 3.4 %fusion.58 = f32[32,32,16]{0,2,1:T(8,128)S(1)} fusion(bf16[16,64,32,32]{1,0,3,2:T(8,128)(2,1)} %reshape.46, bf16[32,32,64]{2,0,1:T(8,128)(2,1)S(1)} %get-tuple-element.316), kind=kOutput, calls=%fused_computation.13.clone.1 | convolution fusion | flops 67125248 | bytes 2293760 | tf_op jit(solution)/shard_map/while/body/eval_jaxpr/ijce,sej->sci/dot_general | solution.py:52
  47.0 0.9 copy.61
  47.8 0.0 reduce-scatter.5.cloned.1.call-update
  47.9 1.3 fusion.56
  49.1 4.7 %copy.60 = bf16[16,64,32,32]{1,0,3,2:T(8,128)(2,1)} copy(bf16[16,64,32,32]{1,2,3,0:T(8,128)(2,1)S(1)} %fusion.56) | data formatting | bytes 4194304 | tf_op jit(solution)/shard_map/while/body/eval_jaxpr/convert_element_type | solution.py:39
  53.8 5.5 %reshape.47 = bf16[1024,1024]{0,1:T(8,128)(2,1)S(1)} reshape(bf16[16,64,32,32]{1,0,3,2:T(8,128)(2,1)} %copy.60) | data formatting | bytes 4194304 | tf_op jit(solution)/shard_map/while/body/eval_jaxpr/reshape | solution.py:39
  59.3 0.0 copy-start
  59.3 0.0 copy-start.2
  59.3 5.7 %fusion.55 = f32[32,32,64]{2,0,1:T(8,128)} fusion(bf16[16,64,32,32]{1,0,3,2:T(8,128)(2,1)} %reshape.46, f32[32,32,64]{2,0,1:T(8,128)} %get-tuple-element.297, pred[]{:T(512)S(6)} %compare.4, bf16[32,32,32]{1,0,2:T(8,128)(2,1)S(1)} %get-tuple-element.313, s32[]{:T(128)S(6)} %select_n.27), kind=kOutput, calls=%fused_computation.9.clone.1 | convolution fusion | flops 67305472 | bytes 2752517 | tf_op jit(solution)/shard_map/while/body/eval_jaxpr/ijce,sci->sej/dot_general | solution.py:57
  65.0 0.0 copy-done
  65.0 0.0 copy-done.2
  65.0 0.7 fusion.57
  65.8 2.7 %reduce-scatter.5.cloned.1.call-done = f32[8,32,16]{1,2,0:T(8,128)} async-done(((f32[32,32,16]{1,2,0:T(8,128)}), f32[8,32,16]{1,2,0:T(8,128)}) %reduce-scatter.5.cloned.1.call-update) | async-done | bytes 16400 | tf_op jit(solution)/shard_map/while/body/eval_jaxpr/reduce_scatter | solution.py:60
  68.5 0.8 constant_dynamic-update-slice_fusion.13
  69.3 0.0 reduce-scatter.5.cloned.1.call-start
  69.3 1.0 constant_dynamic-slice_fusion.3
  70.3 3.0 %convolution_convert_fusion.2 = bf16[1024,1024]{1,0:T(8,128)(2,1)} fusion(bf16[1024,128]{1,0:T(8,128)(2,1)S(1)} %bitcast.82, bf16[1024,128]{1,0:T(8,128)(2,1)} %get-tuple-element.315), kind=kOutput, calls=%fused_computation.4.clone.1 | convolution fusion | flops 269484032 | bytes 2621440 | tf_op jit(solution)/shard_map/while/body/eval_jaxpr/dot_general | solution.py:45
  73.3 2.9 %copy.59 = bf16[1024,1024]{0,1:T(8,128)(2,1)S(1)} copy(bf16[1024,1024]{1,0:T(8,128)(2,1)} %convolution_convert_fusion.2) | data formatting | bytes 4194304 | tf_op jit(solution)/shard_map/while/body/eval_jaxpr/convert_element_type | solution.py:48
  76.2 4.0 %reshape.46 = bf16[16,64,32,32]{1,0,3,2:T(8,128)(2,1)} reshape(bf16[1024,1024]{0,1:T(8,128)(2,1)S(1)} %copy.59) | data formatting | bytes 4194304 | tf_op jit(solution)/shard_map/while/body/eval_jaxpr/reshape | solution.py:48
  80.2 3.4 %fusion.58 = f32[32,32,16]{0,2,1:T(8,128)S(1)} fusion(bf16[16,64,32,32]{1,0,3,2:T(8,128)(2,1)} %reshape.46, bf16[32,32,64]{2,0,1:T(8,128)(2,1)S(1)} %get-tuple-element.316), kind=kOutput, calls=%fused_computation.13.clone.1 | convolution fusion | flops 67125248 | bytes 2293760 | tf_op jit(solution)/shard_map/while/body/eval_jaxpr/ijce,sej->sci/dot_general | solution.py:52
  83.6 0.9 copy.61
  84.5 0.0 reduce-scatter.5.cloned.1.call-update
  84.5 1.3 fusion.56
  85.8 4.7 %copy.60 = bf16[16,64,32,32]{1,0,3,2:T(8,128)(2,1)} copy(bf16[16,64,32,32]{1,2,3,0:T(8,128)(2,1)S(1)} %fusion.56) | data formatting | bytes 4194304 | tf_op jit(solution)/shard_map/while/body/eval_jaxpr/convert_element_type | solution.py:39
  90.5 5.5 %reshape.47 = bf16[1024,1024]{0,1:T(8,128)(2,1)S(1)} reshape(bf16[16,64,32,32]{1,0,3,2:T(8,128)(2,1)} %copy.60) | data formatting | bytes 4194304 | tf_op jit(solution)/shard_map/while/body/eval_jaxpr/reshape | solution.py:39
  96.0 0.0 copy-start
  96.0 0.0 copy-start.2
  96.0 5.8 %fusion.55 = f32[32,32,64]{2,0,1:T(8,128)} fusion(bf16[16,64,32,32]{1,0,3,2:T(8,128)(2,1)} %reshape.46, f32[32,32,64]{2,0,1:T(8,128)} %get-tuple-element.297, pred[]{:T(512)S(6)} %compare.4, bf16[32,32,32]{1,0,2:T(8,128)(2,1)S(1)} %get-tuple-element.313, s32[]{:T(128)S(6)} %select_n.27), kind=kOutput, calls=%fused_computation.9.clone.1 | convolution fusion | flops 67305472 | bytes 2752517 | tf_op jit(solution)/shard_map/while/body/eval_jaxpr/ijce,sci->sej/dot_general | solution.py:57
  101.8 0.0 copy-done
  101.8 0.0 copy-done.2
  101.8 0.7 fusion.57
  102.6 0.3 reduce-scatter.5.cloned.1.call-done
  102.9 0.8 constant_dynamic-update-slice_fusion.13
  103.8 0.0 copy-start.1
  103.8 0.0 reduce-scatter.3.cloned.1.call-start
  103.8 2.3 %copy.37 = f32[32,32,64]{2,1,0:T(8,128)} copy(f32[32,32,64]{2,0,1:T(8,128)} %get-tuple-element.161) | data formatting | bytes 524288 | tf_op jit(solution)/shard_map/while | solution.py:70
  106.1 0.0 reduce-scatter.3.cloned.1.call-update
  106.1 0.8 copy.38
  106.9 33.4 %reduce-scatter.3.cloned.1.call-done = f32[4,32,64]{2,1,0:T(8,128)} async-done(((f32[32,32,64]{2,1,0:T(8,128)}), f32[4,32,64]{2,1,0:T(8,128)}) %reduce-scatter.3.cloned.1.call-update) | async-done | bytes 32784 | tf_op jit(solution)/shard_map/reduce_scatter | solution.py:73
  140.3 0.0 copy-done.1
  (13 shorter events, 0.3 us)
Async XLA Ops:
  8.9 7.4 %collective-permute-start = (bf16[8,32,32]{1,0,2:T(8,128)(2,1)S(1)}, bf16[8,32,32]{1,0,2:T(8,128)(2,1)S(1)}, u32[]{:S(2)}, u32[]{:S(2)}) collective-permute-start(bf16[8,32,32]{1,0,2:T(8,128)(2,1)S(1)} %copy.33), channel_id=1, source_target_pairs={{0,1},{1,2},{2,3},{3,0},{4,5},{5,6},{6,7},{7,4},{8,9},{9,10},{10,1... | collective-permute-start | bytes 49160 | tf_op jit(solution)/shard_map/ppermute | solution.py:12
  16.3 6.1 %collective-permute-start.1 = (bf16[8,32,32]{1,0,2:T(8,128)(2,1)S(1)}, bf16[8,32,32]{1,0,2:T(8,128)(2,1)S(1)}, u32[]{:S(2)}, u32[]{:S(2)}) collective-permute-start(bf16[8,32,32]{1,0,2:T(8,128)(2,1)S(1)} %collective-permute-done), channel_id=1, source_target_pairs={{0,1},{1,2},{2,3},{3,0},{4,5},{5,6},{6,7},{7,4},{8,9},{9,10},{10,1... | collective-permute-start | bytes 49160 | tf_op jit(solution)/shard_map/ppermute | solution.py:12
  22.4 9.8 %collective-permute-start.2 = (bf16[8,32,32]{1,0,2:T(8,128)(2,1)S(1)}, bf16[8,32,32]{1,0,2:T(8,128)(2,1)S(1)}, u32[]{:S(2)}, u32[]{:S(2)}) collective-permute-start(bf16[8,32,32]{1,0,2:T(8,128)(2,1)S(1)} %collective-permute-done.1), channel_id=1, source_target_pairs={{0,1},{1,2},{2,3},{3,0},{4,5},{5,6},{6,7},{7,4},{8,9},{9,10},{10,1... | collective-permute-start | bytes 49160 | tf_op jit(solution)/shard_map/ppermute | solution.py:12
  32.6 35.9 %reduce-scatter.5.cloned.1.call-start = ((), (), s32[]{:S(2)}) async-start(), calls=%async_computation.3 | async-start | bytes 327680 | tf_op jit(solution)/shard_map/while/body/eval_jaxpr/reduce_scatter | solution.py:60
  59.3 5.7 %copy-start = (bf16[1024,128]{1,0:T(8,128)(2,1)S(1)}, bf16[1024,128]{1,0:T(8,128)(2,1)}, u32[]{:S(2)}) copy-start(bf16[1024,128]{1,0:T(8,128)(2,1)} %get-tuple-element.315) | copy-start | bytes 786436 | tf_op jit(solution)/shard_map/while
  59.3 5.7 %copy-start.2 = (f32[128]{0:T(128)S(1)}, f32[128]{0:T(128)}, u32[]{:S(2)}) copy-start(f32[128]{0:T(128)} %get-tuple-element.317) | copy-start | bytes 1540 | tf_op jit(solution)/shard_map/while
  69.3 33.6 %reduce-scatter.5.cloned.1.call-start = ((), (), s32[]{:S(2)}) async-start(), calls=%async_computation.3 | async-start | bytes 327680 | tf_op jit(solution)/shard_map/while/body/eval_jaxpr/reduce_scatter | solution.py:60
  96.0 5.8 %copy-start = (bf16[1024,128]{1,0:T(8,128)(2,1)S(1)}, bf16[1024,128]{1,0:T(8,128)(2,1)}, u32[]{:S(2)}) copy-start(bf16[1024,128]{1,0:T(8,128)(2,1)} %get-tuple-element.315) | copy-start | bytes 786436 | tf_op jit(solution)/shard_map/while
  96.0 5.8 %copy-start.2 = (f32[128]{0:T(128)S(1)}, f32[128]{0:T(128)}, u32[]{:S(2)}) copy-start(f32[128]{0:T(128)} %get-tuple-element.317) | copy-start | bytes 1540 | tf_op jit(solution)/shard_map/while
  103.8 36.5 %copy-start.1 = (bf16[32,64,128]{2,1,0:T(8,128)(2,1)}, bf16[32,64,128]{2,1,0:T(8,128)(2,1)S(1)}, u32[]{:S(2)}) copy-start(bf16[32,64,128]{2,1,0:T(8,128)(2,1)S(1)} %get-tuple-element.207) | copy-start | bytes 1572868
  103.8 36.5 %reduce-scatter.3.cloned.1.call-start = ((), (), s32[]{:S(2)}) async-start(), calls=%async_computation.2 | async-start | bytes 589824 | tf_op jit(solution)/shard_map/reduce_scatter | solution.py:73
Sparse Core Ops, SparseCore 0:
  48.0 20.4 reduce-scatter.4
  84.6 18.2 reduce-scatter.4
Sparse Core Ops, SparseCore 1:
  107.9 32.3 reduce-scatter.2
